TPU v7x, 32 devices: a whole 2x2x4 slice. The times are simulated.
32 devices in a mesh: dom: 32 (over z, y, x, core).
Axes of the slice: x: 2, y: 2, z: 4, core: 2. Of those that a mesh axis runs over, the one named last changes fastest.
Arguments:
- traction: float32 [16384, 3, 128], P('dom'), may hold values from -6 to 6
- fluid_coords: float32 [16384, 3, 128], P('dom'), may hold values from 0 to 1
- struct_coords: float32 [3, 32, 4096], P(None, None, 'dom'), may hold values from 0 to 1
- dest: int32 [16384, 1], P('dom'), may hold values from 0 to 31; in each aligned block of 512 rows (0 to 511, 512 to 1023, ...) at most 32 rows name the same one
- target: int32 [16384], P('dom'), may hold values from 0 to 127
- blocks: float32 [3, 96, 96, 4096], P(None, None, None, 'dom'), may hold values from -1 to 7, as said below
- columns: int32 [2, 4096], P(None, 'dom'), may hold values from 0 to 159
- halo_list: int32 [512], P('dom'), may hold values from 0 to 127
- precond: float32 [96, 96, 4096], P(None, None, 'dom'), may hold values from -1 to 1
Outputs:
- load_field: float32 [96, 4096], P(None, 'dom')
- solution: float32 [96, 4096], P(None, 'dom')
- residual: float32 [96, 4096], P(None, 'dom')
Inputs may be any that keep to these rules, and one draw needn't show every extreme that they name: `dest`: among the fluid blocks of one partition no partition is named more than 32 times, a bound that some block reaches. Each diagonal block is its positive diagonal plus small full entries; coupling blocks are small full blocks.
All inputs are finite; a program needn't handle non-finite values.
Results may differ from a plain program's by a relative error of at most 0.0003.
Values sent between devices are 32-bit elements; how exact they have to be, the bound alone decides.
A program may use at most 128 MiB of HBM per device.

v0:
```python
import jax
import jax.numpy as jnp
from jax import lax
from jax.sharding import PartitionSpec as P

ITERS = 2


support = 0.9


def from_behind(block, axis, distance):
    devices = range(lax.axis_size(axis))
    route = [(i - distance, i) for i in devices if i - distance in devices]
    return lax.ppermute(block, axis, route)


def wendland_map(fluid_pos, force, struct_pos):
    dist_sq = jnp.zeros((fluid_pos.shape[0], struct_pos.shape[2], fluid_pos.shape[2]), jnp.float32)
    for component in range(3):
        dist_sq = (
            dist_sq + (struct_pos[:, component, :, None] - fluid_pos[:, component, None, :]) ** 2
        )
    radius = jnp.sqrt(dist_sq) / support
    weight = jnp.maximum(1.0 - radius, 0.0) ** 4 * (4.0 * radius + 1.0)
    mapped = jnp.einsum("bjn,bcn->bcj", weight, force, precision=lax.Precision.HIGHEST)
    return mapped.reshape(mapped.shape[0], -1)


def precondition(precond, vector):
    return jnp.einsum("abi,bi->ai", precond, vector, precision=lax.Precision.HIGHEST)


def apply_operator(vector, blocks, columns, halo_list):
    outgoing = jnp.take(vector, halo_list, axis=1)
    from_left = from_behind(outgoing, "dom", 1)
    from_right = from_behind(outgoing, "dom", -1)
    extended = jnp.concatenate([vector, from_left, from_right], axis=1)
    result = jnp.einsum("abi,bi->ai", blocks[0], vector, precision=lax.Precision.HIGHEST)
    for neighbor in range(columns.shape[0]):
        taken = jnp.take(extended, columns[neighbor], axis=1)
        result = result + jnp.einsum(
            "abi,bi->ai", blocks[neighbor + 1], taken, precision=lax.Precision.HIGHEST
        )
    return result


def on_device(
    traction, fluid_coords, struct_coords, dest, target, blocks, columns, halo_list, precond
):
    partitions = lax.axis_size("dom")
    fluid_count = dest.shape[0]
    cluster = blocks.shape[1]
    local_blocks = blocks.shape[3]
    capacity = max(2, 2 * fluid_count // partitions)
    owner_part = dest[:, 0]
    owner_hits = (owner_part[:, None] == jnp.arange(partitions, dtype=jnp.int32)[None, :]).astype(
        jnp.int32
    )
    before = jnp.sum((jnp.cumsum(owner_hits, axis=0) - owner_hits) * owner_hits, axis=1)
    slot_index = owner_part * capacity + before
    slot_target = jnp.zeros((partitions * capacity,), jnp.int32).at[slot_index].set(target)
    slot_target = slot_target.reshape(partitions, capacity)
    all_struct = lax.all_gather(struct_coords, "dom", axis=2, tiled=True)
    global_index = owner_part * local_blocks + target
    struct_pos = jnp.transpose(jnp.take(all_struct, global_index, axis=2), (2, 0, 1))
    mapped = wendland_map(fluid_coords, traction, struct_pos)
    outgoing = jnp.zeros((partitions * capacity, cluster), jnp.float32).at[slot_index].set(mapped)
    outgoing = outgoing.reshape(partitions, capacity, cluster)
    arrived, labels = (
        lax.all_to_all(outgoing, "dom", split_axis=0, concat_axis=0, tiled=True),
        lax.all_to_all(slot_target, "dom", split_axis=0, concat_axis=0, tiled=True),
    )
    onehot = (
        labels.reshape(-1)[:, None] == jnp.arange(local_blocks, dtype=jnp.int32)[None, :]
    ).astype(jnp.float32)
    load_field = jnp.dot(
        arrived.reshape(-1, cluster).T,
        onehot,
        precision=lax.Precision.HIGHEST,
        preferred_element_type=jnp.float32,
    )
    solution = jnp.zeros_like(load_field)
    residual = load_field
    search = load_field
    alignment = lax.psum(jnp.sum(load_field * residual), "dom")
    for step in range(ITERS):
        search_pre = precondition(precond, search)
        image = apply_operator(search_pre, blocks, columns, halo_list)
        step_size = alignment / lax.psum(jnp.sum(load_field * image), "dom")
        middle = residual - step_size * image
        middle_pre = precondition(precond, middle)
        middle_image = apply_operator(middle_pre, blocks, columns, halo_list)
        crossed, squared = lax.psum(
            (jnp.sum(middle_image * middle), jnp.sum(middle_image * middle_image)), "dom"
        )
        smoothing = crossed / squared
        solution = solution + step_size * search_pre + smoothing * middle_pre
        residual = middle - smoothing * middle_image
        new_alignment = lax.psum(jnp.sum(load_field * residual), "dom")
        momentum = new_alignment / alignment * (step_size / smoothing)
        search = residual + momentum * (search - smoothing * image)
        alignment = new_alignment
    return (load_field, solution, residual)


def solution(mesh):
    return jax.shard_map(
        on_device,
        mesh=mesh,
        in_specs=(
            P("dom", None, None),
            P("dom", None, None),
            P(None, None, "dom"),
            P("dom", None),
            P("dom"),
            P(None, None, None, "dom"),
            P(None, "dom"),
            P("dom"),
            P(None, None, "dom"),
        ),
        out_specs=(P(None, "dom"), P(None, "dom"), P(None, "dom")),
        check_vma=False,
    )
```

profile of v0, /device:TPU:0, one launch (start us, length us, event | category | flops | bytes accessed | tf_op | source)
XLA Modules:
  0.0 430.5 jit_solution(12812024123034165464)
XLA Ops:
  7.2 0.7 all-gather.2.cloned.1.call-update
  7.9 0.7 fusion.51
  8.6 1.2 reduce-window.6
  10.0 0.8 fusion.50
  10.8 0.7 compare_select_fusion
  11.5 2.6 scatter_custom_fusion.1
  14.1 0.7 all_to_all.10
  14.8 7.3 %all-to-all-start.1 = ((s32[32,1,32]{2,1,0:T(1,128)}), s32[32,1,32]{2,1,0:T(1,128)S(1)}, u32[]{:S(2)}, u32[]{:S(2)}) async-start(s32[32,1,32]{2,1,0:T(1,128)} %all_to_all.10), calls=%async_computation.1 | async-start | bytes 32768 | tf_op jit(solution)/shard_map/all_to_all | solution.py:72
  22.1 0.7 compare_and_fusion.3
  22.9 1.2 slice_bitcast_fusion.2
  24.0 44.0 %all-gather.2.cloned.1.call-done = f32[3,32,4096]{2,1,0:T(8,128)} async-done(((f32[3,32,128]{2,1,0:T(8,128)}), f32[3,32,4096]{2,1,0:T(8,128)}) %all-gather.2.cloned.1.call-update) | async-done | bytes 1572880 | tf_op jit(solution)/shard_map/all_gather | solution.py:64
  68.0 7.2 %copy.127 = f32[3,32,4096]{1,0,2:T(4,128)} copy(f32[3,32,4096]{2,1,0:T(8,128)} %all-gather.2.cloned.1.call-done) | data formatting | bytes 3145728 | tf_op jit(solution)/shard_map/all_gather | solution.py:64
  75.2 4.9 %gather_fusion = f32[512,3,32]{2,1,0:T(4,128)S(1)} fusion(f32[3,32,4096]{1,0,2:T(4,128)} %copy.127, s32[1024]{0:T(1024)S(1)} %pad_clamp_fusion.3), kind=kCustom, calls=%fused_computation.12 | custom fusion | bytes 395264 | tf_op jit(solution)/shard_map/jit(_take)/gather | solution.py:66
  80.1 1.8 broadcast_select_fusion
  82.4 22.2 %fusion.40 = f32[512,3,32]{2,1,0:T(4,128)S(1)} fusion(f32[512,128]{1,0:T(8,128)S(1)} %get-tuple-element.42, f32[512,32]{1,0:T(8,128)S(1)} %bitcast.242, f32[512,128]{1,0:T(8,128)S(1)} %get-tuple-element.43, f32[512,32]{1,0:T(8,128)S(1)} %bitcast.241, f32[512,128]{1,0:T(8,128)S(1)} %get-tuple-element.41, f32[512,32]{1,0:T(8,128)S(1)} %bitcast.240, ...), kind=kOutput, calls=%fused_computation.71 | convolution fusion | flops 109051904 | bytes 1966080 | tf_op jit(solution)/shard_map/bjn,bcn->bcj/dot_general | solution.py:26
  105.0 2.5 scatter_custom_fusion
  107.5 3.5 all-to-all-start
  111.6 0.7 reduce.37
  112.4 14.2 %all-to-all-done = f32[32,32,96]{2,1,0:T(8,128)S(1)} async-done(((f32[32,32,96]{2,1,0:T(8,128)}), f32[32,32,96]{2,1,0:T(8,128)S(1)}, u32[]{:S(2)}, u32[]{:S(2)}) %all-to-all-start) | async-done | bytes 393248 | tf_op jit(solution)/shard_map/all_to_all | solution.py:71
  126.6 0.7 fusion.44
  127.4 3.1 multiply_reduce_fusion.3
  131.3 1.8 collective-permute-start
  133.0 1.3 collective-permute-start.1
  134.4 2.2 collective-permute-done.1
  137.8 0.7 gather_fusion.2
  138.6 6.2 %fusion.22 = (f32[128,96]{0,1:T(8,128)S(1)}, f32[128,96]{0,1:T(8,128)S(1)}, f32[128,96]{0,1:T(8,128)S(1)}) fusion(f32[3,96,96,128]{3,2,1,0:T(8,128)} %param.18, f32[128,96]{0,1:T(8,128)S(1)} %copy.258, f32[128,96]{0,1:T(8,128)S(1)} %multiply_reduce_fusion.3, f32[128,96]{0,1:T(8,128)S(1)} %copy.259), kind=kLoop, calls=%fused_computation.45 | loop fusion | flops 7041024 | bytes 14450688 | tf_op jit(solution)/shard_map/abi,bi->ai/dot_general | solution.py:42
  145.5 42.6 %all-reduce.2 = (f32[]{:T(128)}, f32[]{:T(128)}) all-reduce(f32[]{:T(128)} %get-tuple-element.22, f32[]{:T(128)} %get-tuple-element.21), channel_id=1, replica_groups=mesh['dom'=32] {'dom'}, use_global_device_ids=true, to_apply=%region_6.7 | all-reduce | flops 2 | bytes 16 | tf_op jit(solution)/shard_map/psum | solution.py:86
  189.4 3.1 multiply_reduce_fusion.2
  193.3 1.3 collective-permute-start.2
  194.6 1.3 collective-permute-start.3
  196.0 4.2 collective-permute-done.3
  202.1 6.2 %fusion.23 = (f32[128,96]{0,1:T(8,128)S(1)}, f32[128,96]{0,1:T(8,128)S(1)}, f32[128,96]{0,1:T(8,128)S(1)}) fusion(f32[3,96,96,128]{3,2,1,0:T(8,128)} %param.18, f32[128,96]{0,1:T(8,128)S(1)} %copy.263, f32[128,96]{0,1:T(8,128)S(1)} %multiply_reduce_fusion.2, f32[128,96]{0,1:T(8,128)S(1)} %copy.264), kind=kLoop, calls=%fused_computation.46 | loop fusion | flops 7041024 | bytes 14450688 | tf_op jit(solution)/shard_map/abi,bi->ai/dot_general | solution.py:42
  208.3 0.7 fusion.58
  209.0 41.9 %all-reduce.1 = (f32[]{:T(128)}, f32[]{:T(128)}) all-reduce(f32[]{:T(128)} %get-tuple-element.20, f32[]{:T(128)} %get-tuple-element.19), channel_id=1, replica_groups=mesh['dom'=32] {'dom'}, use_global_device_ids=true, to_apply=%region_10.13 | all-reduce | flops 2 | bytes 16 | tf_op jit(solution)/shard_map/psum | solution.py:94
  255.4 40.3 %psum.60 = f32[]{:T(128)} all-reduce(f32[]{:T(128)} %multiply_reduce_fusion.4), channel_id=1, replica_groups=mesh['dom'=32] {'dom'}, use_global_device_ids=true, to_apply=%region_14.17 | all-reduce | flops 1 | bytes 8 | tf_op jit(solution)/shard_map/psum | solution.py:100
  297.1 3.1 multiply_reduce_fusion.1
  301.0 1.3 collective-permute-start.4
  302.3 1.3 collective-permute-start.5
  303.7 4.2 collective-permute-done.5
  309.8 6.2 %fusion.24 = (f32[128,96]{0,1:T(8,128)S(1)}, f32[128,96]{0,1:T(8,128)S(1)}, f32[128,96]{0,1:T(8,128)S(1)}) fusion(f32[3,96,96,128]{3,2,1,0:T(8,128)} %param.18, f32[128,96]{0,1:T(8,128)S(1)} %copy.268, f32[128,96]{0,1:T(8,128)S(1)} %multiply_reduce_fusion.1, f32[128,96]{0,1:T(8,128)S(1)} %copy.269), kind=kLoop, calls=%fused_computation.47 | loop fusion | flops 7041024 | bytes 14450688 | tf_op jit(solution)/shard_map/abi,bi->ai/dot_general | solution.py:42
  316.6 41.5 %psum.61 = f32[]{:T(128)} all-reduce(f32[]{:T(128)} %fusion.55), channel_id=1, replica_groups=mesh['dom'=32] {'dom'}, use_global_device_ids=true, to_apply=%region_16.19 | all-reduce | flops 1 | bytes 8 | tf_op jit(solution)/shard_map/psum | solution.py:90
  359.5 3.1 multiply_reduce_fusion
  363.3 1.3 collective-permute-start.6
  364.6 1.3 collective-permute-start.7
  366.0 4.2 collective-permute-done.7
  370.5 0.7 gather_fusion.11
  372.0 6.2 %fusion.25 = (f32[128,96]{0,1:T(8,128)S(1)}, f32[128,96]{0,1:T(8,128)S(1)}, f32[128,96]{0,1:T(8,128)S(1)}) fusion(f32[3,96,96,128]{3,2,1,0:T(8,128)} %param.18, f32[128,96]{0,1:T(8,128)S(1)} %copy.273, f32[128,96]{0,1:T(8,128)S(1)} %multiply_reduce_fusion, f32[128,96]{0,1:T(8,128)S(1)} %copy.274), kind=kLoop, calls=%fused_computation.48 | loop fusion | flops 7041024 | bytes 14450688 | tf_op jit(solution)/shard_map/abi,bi->ai/dot_general | solution.py:42
  378.9 42.2 %all-reduce = (f32[]{:T(128)}, f32[]{:T(128)}) all-reduce(f32[]{:T(128)} %get-tuple-element.18, f32[]{:T(128)} %get-tuple-element.17), channel_id=1, replica_groups=mesh['dom'=32] {'dom'}, use_global_device_ids=true, to_apply=%region_18.21 | all-reduce | flops 2 | bytes 16 | tf_op jit(solution)/shard_map/psum | solution.py:94
  (87 shorter events, 15.1 us)
Async XLA Ops:
  7.2 75.2 %copy-start = (f32[512,3,128]{2,0,1:T(8,128)S(1)}, f32[512,3,128]{2,0,1:T(8,128)}, u32[]{:S(2)}) copy-start(f32[512,3,128]{2,0,1:T(8,128)} %param.13) | copy-start | bytes 2359300
  7.2 60.8 %all-gather.2.cloned.1.call-start = ((), (), s32[]{:S(2)}) async-start(), calls=%async_computation.2 | async-start | bytes 1622016 | tf_op jit(solution)/shard_map/all_gather | solution.py:64
  14.8 92.7 %all-to-all-start.1 = ((s32[32,1,32]{2,1,0:T(1,128)}), s32[32,1,32]{2,1,0:T(1,128)S(1)}, u32[]{:S(2)}, u32[]{:S(2)}) async-start(s32[32,1,32]{2,1,0:T(1,128)} %all_to_all.10), calls=%async_computation.1 | async-start | bytes 32768 | tf_op jit(solution)/shard_map/all_to_all | solution.py:72
  82.4 28.6 %copy-start.3 = (s32[16]{0:T(128)S(1)}, s32[16]{0:T(128)}, u32[]{:S(2)}) copy-start(s32[16]{0:T(128)} %param.20) | copy-start | bytes 196
  82.4 28.7 %copy-start.2 = (s32[2,128]{1,0:T(2,128)S(1)}, s32[2,128]{1,0:T(2,128)}, u32[]{:S(2)}) copy-start(s32[2,128]{1,0:T(2,128)} %param.19) | copy-start | bytes 3076
  107.5 19.1 %all-to-all-start = ((f32[32,32,96]{2,1,0:T(8,128)}), f32[32,32,96]{2,1,0:T(8,128)S(1)}, u32[]{:S(2)}, u32[]{:S(2)}) async-start(f32[32,32,96]{2,1,0:T(8,128)} %bitcast.45), calls=%async_computation | async-start | bytes 1048576 | tf_op jit(solution)/shard_map/all_to_all | solution.py:71
  127.4 232.1 %copy-start.1 = (f32[96,128]{1,0:T(8,128)}, f32[96,128]{1,0:T(8,128)S(1)}, u32[]{:S(2)}) copy-start(f32[96,128]{1,0:T(8,128)S(1)} %fusion.44) | copy-start | bytes 147460
  131.3 3.1 collective-permute-start
  133.0 3.6 collective-permute-start.1
  193.3 2.6 collective-permute-start.2
  194.6 5.6 %collective-permute-start.3 = (f32[96,16]{0,1:T(8,128)S(1)}, f32[96,16]{0,1:T(8,128)S(1)}, u32[]{:S(2)}, u32[]{:S(2)}) collective-permute-start(f32[96,16]{0,1:T(8,128)S(1)} %select_bitcast_fusion.2), channel_id=1, source_target_pairs={{1,0},{2,1},{3,2},{4,3},{5,4},{6,5},{7,6},{8,7},{9,8},{10,9},{11,1... | collective-permute-start | bytes 18440 | tf_op jit(solution)/shard_map/ppermute | solution.py:15
  301.0 2.6 collective-permute-start.4
  302.3 5.6 %collective-permute-start.5 = (f32[96,16]{0,1:T(8,128)S(1)}, f32[96,16]{0,1:T(8,128)S(1)}, u32[]{:S(2)}, u32[]{:S(2)}) collective-permute-start(f32[96,16]{0,1:T(8,128)S(1)} %select_bitcast_fusion.1), channel_id=1, source_target_pairs={{1,0},{2,1},{3,2},{4,3},{5,4},{6,5},{7,6},{8,7},{9,8},{10,9},{11,1... | collective-permute-start | bytes 18440 | tf_op jit(solution)/shard_map/ppermute | solution.py:15
  363.3 2.6 collective-permute-start.6
  364.6 5.6 %collective-permute-start.7 = (f32[96,16]{0,1:T(8,128)S(1)}, f32[96,16]{0,1:T(8,128)S(1)}, u32[]{:S(2)}, u32[]{:S(2)}) collective-permute-start(f32[96,16]{0,1:T(8,128)S(1)} %select_bitcast_fusion), channel_id=1, source_target_pairs={{1,0},{2,1},{3,2},{4,3},{5,4},{6,5},{7,6},{8,7},{9,8},{10,9},{11,1... | collective-permute-start | bytes 18440 | tf_op jit(solution)/shard_map/ppermute | solution.py:15
Sparse Core Ops, SparseCore 0:
  10.9 57.0 all-gather.1
where the time goes:
time: 432 us; the launch traced here: 431 us
  blocking collectives  208 us (48%)
  waiting for transfers between devices  73.7 us (17%)
  other arithmetic  49.7 us (12%)
  local copies, waits for them, and re-layouts  30.3 us (7%)
  between operations  23.9 us (6%)
  matrix products  22.9 us (5%)
  starting transfers between devices  21.6 us (5%)
    psum x2, blocking collectives, on_device(): lax.psum((jnp.sum(middle_image * middle), jnp.sum(middle_image * middle_i...  84 us
    all_gather x1, waiting for transfers between devices, on_device(): all_struct = lax.all_gather(struct_coords, 'dom', axis=2, tiled=True)  44 us
    psum x1, blocking collectives, on_device(): alignment = lax.psum(jnp.sum(load_field * residual), 'dom')  42.6 us
    psum x1, blocking collectives, on_device(): step_size = alignment / lax.psum(jnp.sum(load_field * image), 'dom')  41.5 us
    psum x1, blocking collectives, on_device(): new_alignment = lax.psum(jnp.sum(load_field * residual), 'dom')  40.3 us
    dot_general x4, other arithmetic, apply_operator(): jnp.einsum('abi,bi->ai', blocks[neighbor + 1], taken, precision=lax.Preci...  24.9 us
    dot_general x1, matrix products, wendland_map(): jnp.einsum('bjn,bcn->bcj', weight, force, precision=lax.Precision.HIGHEST)  22.2 us
    ppermute x8, waiting for transfers between devices, from_behind(): return lax.ppermute(block, axis, route)  14.8 us
  transfers between devices with their start and end apart: 11, of which 6 were waited for; matrix products, arithmetic and copies ran while one was open for 11% of the time, Pallas kernels for 0%

commit v1 on v0

v1 whole, which is shorter than its diff:
```python
import functools

import jax
import jax.numpy as jnp
from jax import lax
from jax.experimental import pallas as pl
from jax.experimental.pallas import tpu as pltpu
from jax.sharding import PartitionSpec as P

support = 0.9


def wendland_map(fluid_pos, force, struct_pos):
    dist_sq = jnp.zeros((fluid_pos.shape[0], struct_pos.shape[2], fluid_pos.shape[2]), jnp.float32)
    for component in range(3):
        dist_sq = (
            dist_sq + (struct_pos[:, component, :, None] - fluid_pos[:, component, None, :]) ** 2
        )
    radius = jnp.sqrt(dist_sq) / support
    weight = jnp.maximum(1.0 - radius, 0.0) ** 4 * (4.0 * radius + 1.0)
    mapped = jnp.einsum("bjn,bcn->bcj", weight, force, precision=lax.Precision.HIGHEST)
    return mapped.reshape(mapped.shape[0], -1)


def split_three(x):
    high = x.astype(jnp.bfloat16)
    rest = x - high.astype(jnp.float32)
    mid = rest.astype(jnp.bfloat16)
    low = (rest - mid.astype(jnp.float32)).astype(jnp.bfloat16)
    return high, mid, low


def pick(pieces, onehot, dims):
    total = None
    for piece in pieces:
        part = lax.dot_general(
            piece, onehot, (dims, ((), ())), preferred_element_type=jnp.float32
        )
        total = part if total is None else total + part
    return total


def krylov_kernel(
    parts,
    load_ref,
    columns_ref,
    halo_ref,
    blocks_hbm,
    precond_hbm,
    solution_ref,
    residual_ref,
    blocks,
    precond,
    operand,
    taken,
    spare,
    halo_out,
    halo_in,
    partial,
    load_sems,
    halo_send,
    halo_recv,
    sum_send,
    sum_recv,
):
    me = lax.axis_index("dom")
    cluster, local = load_ref.shape
    listed = halo_ref.shape[0]
    barrier = pltpu.get_barrier_semaphore()

    loads = [pltpu.make_async_copy(precond_hbm, precond, load_sems.at[0])]
    for which in range(3):
        loads.append(
            pltpu.make_async_copy(
                blocks_hbm.at[which], blocks.at[which], load_sems.at[which + 1]
            )
        )
    for copy in loads:
        copy.start()

    @pl.loop(1, parts)
    def _(k):
        pl.semaphore_signal(
            barrier, 1, device_id=(lax.rem(me + k, parts),), device_id_type=pl.DeviceIdType.MESH
        )

    columns = columns_ref[...]
    rows = lax.broadcasted_iota(jnp.int32, (local, local), 0)
    rim = lax.broadcasted_iota(jnp.int32, (listed, local), 0)

    def hot(cond):
        return jnp.where(cond, 1.0, 0.0).astype(jnp.bfloat16)

    own_hot = [hot(rows == columns[k : k + 1, :]) for k in range(2)]
    left_hot = [hot(rim + local == columns[k : k + 1, :]) for k in range(2)]
    right_hot = [hot(rim + (local + listed) == columns[k : k + 1, :]) for k in range(2)]
    own_hot = jnp.concatenate(own_hot, axis=1)
    left_hot = jnp.concatenate(left_hot, axis=1)
    right_hot = jnp.concatenate(right_hot, axis=1)
    send_hot = hot(lax.broadcasted_iota(jnp.int32, (listed, local), 1) == halo_ref[...])

    group = 8

    def multiply(matrices, vectors, out_ref):
        @pl.loop(0, cluster // group)
        def _(g):
            start = pl.multiple_of(g * group, group)
            for row in range(group):
                total = None
                for matrix, vector in zip(matrices, vectors):
                    term = matrix[pl.ds(start + row, 1)][0] * vector[...]
                    total = term if total is None else total + term
                spare[row : row + 1, :] = jnp.sum(total, axis=0, keepdims=True)
            out_ref[pl.ds(start, group), :] = spare[...]

    def halo_copy(step, side):
        peer = me + 1 if side == 0 else me - 1
        return pltpu.make_async_remote_copy(
            src_ref=halo_out.at[step],
            dst_ref=halo_in.at[step, side],
            send_sem=halo_send.at[step, side],
            recv_sem=halo_recv.at[step, side],
            device_id=(peer,),
            device_id_type=pl.DeviceIdType.MESH,
        )

    def apply(step, vector):
        operand[0] = vector
        if step == 0:
            loads[0].wait()
        multiply([precond], [operand.at[0]], operand.at[1])
        pre = operand[1]
        pieces = split_three(pre)
        outgoing = None
        for piece in pieces:
            part = lax.dot_general(
                send_hot, piece, (((1,), (1,)), ((), ())), preferred_element_type=jnp.float32
            )
            outgoing = part if outgoing is None else outgoing + part
        halo_out[step] = outgoing
        if step == 0:
            pl.semaphore_wait(barrier, parts - 1)

        @pl.when(me < parts - 1)
        def _():
            halo_copy(step, 0).start()

        @pl.when(me > 0)
        def _():
            halo_copy(step, 1).start()

        near = pick(pieces, own_hot, ((1,), (0,)))
        if step == 0:
            for copy in loads[1:]:
                copy.wait()

        @pl.when(me < parts - 1)
        def _():
            halo_copy(step, 0).wait_send()
            halo_copy(step, 1).wait_recv()

        @pl.when(me > 0)
        def _():
            halo_copy(step, 1).wait_send()
            halo_copy(step, 0).wait_recv()

        left = jnp.where(me > 0, halo_in[step, 0], 0.0)
        right = jnp.where(me < parts - 1, halo_in[step, 1], 0.0)
        near = near + pick(split_three(left), left_hot, ((0,), (0,)))
        near = near + pick(split_three(right), right_hot, ((0,), (0,)))
        taken[0] = near[:, :local]
        taken[1] = near[:, local:]
        multiply(
            [blocks.at[0], blocks.at[1], blocks.at[2]],
            [operand.at[1], taken.at[0], taken.at[1]],
            operand.at[2],
        )
        return pre, operand[2]

    lanes = lax.broadcasted_iota(jnp.int32, (1, local), 1)

    def sum_copy(turn, source, target):
        return pltpu.make_async_remote_copy(
            src_ref=partial.at[turn, source],
            dst_ref=partial.at[turn, source],
            send_sem=sum_send.at[turn, target],
            recv_sem=sum_recv.at[turn, source],
            device_id=(target,),
            device_id_type=pl.DeviceIdType.MESH,
        )

    def sums(turn, pairs):
        packed = jnp.zeros((1, local), jnp.float32)
        for index, (x, y) in enumerate(pairs):
            value = jnp.sum(jnp.sum(x * y, axis=0, keepdims=True), axis=1, keepdims=True)
            packed = jnp.where(lanes == index, value, packed)
        partial[turn, me] = packed

        @pl.loop(1, parts)
        def _(k):
            sum_copy(turn, me, lax.rem(me + k, parts)).start()

        @pl.loop(1, parts)
        def _(k):
            other = lax.rem(me + k, parts)
            sum_copy(turn, other, other).wait_recv()
            sum_copy(turn, me, other).wait_send()

        total = jnp.sum(partial[turn], axis=0)
        return [
            jnp.sum(jnp.where(lanes == index, total, 0.0), axis=1, keepdims=True)
            for index in range(len(pairs))
        ]

    v0 = load_ref[...]
    z0, v1 = apply(0, v0)
    z1, v2 = apply(1, v1)
    g00, g01, g02, g11, g12, g22 = sums(
        0, [(v0, v0), (v0, v1), (v0, v2), (v1, v1), (v1, v2), (v2, v2)]
    )
    step_size = g00 / g01
    crossed = g01 - step_size * (g02 + g11) + step_size * step_size * g12
    squared = g11 - 2.0 * step_size * g12 + step_size * step_size * g22
    smoothing = crossed / squared
    solution = step_size * z0 + smoothing * (z0 - step_size * z1)
    residual = (v0 - step_size * v1) - smoothing * (v1 - step_size * v2)
    alignment = (g00 - step_size * g01) - smoothing * (g01 - step_size * g02)
    momentum = (alignment / g00) * (step_size / smoothing)
    search = residual + momentum * (v0 - smoothing * v1)
    p0, image = apply(2, search)
    p1, y = apply(3, image)
    q = image - momentum * (v1 - smoothing * v2)
    pre = p0 - momentum * (z0 - smoothing * z1)
    sr, si, qr, qi, yr, yi, qq, qy, yy = sums(
        1,
        [
            (v0, residual),
            (v0, image),
            (q, residual),
            (q, image),
            (y, residual),
            (y, image),
            (q, q),
            (q, y),
            (y, y),
        ],
    )
    step_size = sr / si
    crossed = qr - step_size * (qi + yr) + step_size * step_size * yi
    squared = qq - 2.0 * step_size * qy + step_size * step_size * yy
    smoothing = crossed / squared
    solution_ref[...] = solution + step_size * p0 + smoothing * (pre - step_size * p1)
    residual_ref[...] = (residual - step_size * image) - smoothing * (q - step_size * y)


def krylov(load_field, columns, halo_list, blocks, precond):
    parts = lax.axis_size("dom")
    cluster, local = load_field.shape
    listed = halo_list.shape[0]
    vmem = pl.BlockSpec(memory_space=pltpu.VMEM)
    hbm = pl.BlockSpec(memory_space=pl.ANY)
    field = jax.ShapeDtypeStruct((cluster, local), jnp.float32)
    f32 = jnp.float32
    return pl.pallas_call(
        functools.partial(krylov_kernel, parts),
        out_shape=(field, field),
        in_specs=[vmem, vmem, vmem, hbm, hbm],
        out_specs=(vmem, vmem),
        scratch_shapes=[
            pltpu.VMEM(blocks.shape, f32),
            pltpu.VMEM(precond.shape, f32),
            pltpu.VMEM((3, cluster, local), f32),
            pltpu.VMEM((2, cluster, local), f32),
            pltpu.VMEM((8, local), f32),
            pltpu.VMEM((4, listed, cluster), f32),
            pltpu.VMEM((4, 2, listed, cluster), f32),
            pltpu.VMEM((2, parts, 1, local), f32),
            pltpu.SemaphoreType.DMA((4,)),
            pltpu.SemaphoreType.DMA((4, 2)),
            pltpu.SemaphoreType.DMA((4, 2)),
            pltpu.SemaphoreType.DMA((2, parts)),
            pltpu.SemaphoreType.DMA((2, parts)),
        ],
        compiler_params=pltpu.CompilerParams(collective_id=0, has_side_effects=True),
        name="krylov",
    )(load_field, columns, halo_list.reshape(-1, 1), blocks, precond)


def on_device(
    traction, fluid_coords, struct_coords, dest, target, blocks, columns, halo_list, precond
):
    partitions = lax.axis_size("dom")
    fluid_count = dest.shape[0]
    cluster = blocks.shape[1]
    local_blocks = blocks.shape[3]
    capacity = max(2, 2 * fluid_count // partitions)
    owner_part = dest[:, 0]
    owner_hits = (owner_part[:, None] == jnp.arange(partitions, dtype=jnp.int32)[None, :]).astype(
        jnp.int32
    )
    before = jnp.sum((jnp.cumsum(owner_hits, axis=0) - owner_hits) * owner_hits, axis=1)
    slot_index = owner_part * capacity + before
    slot_target = jnp.zeros((partitions * capacity,), jnp.int32).at[slot_index].set(target)
    slot_target = slot_target.reshape(partitions, capacity)
    labels = lax.all_to_all(slot_target, "dom", split_axis=0, concat_axis=0, tiled=True)
    onehot = (
        labels.reshape(-1)[:, None] == jnp.arange(local_blocks, dtype=jnp.int32)[None, :]
    ).astype(jnp.float32)
    asked = jnp.dot(
        onehot,
        struct_coords.reshape(-1, local_blocks).T,
        precision=lax.Precision.HIGHEST,
        preferred_element_type=jnp.float32,
    )
    answers = lax.all_to_all(
        asked.reshape(partitions, capacity, cluster),
        "dom",
        split_axis=0,
        concat_axis=0,
        tiled=True,
    )
    answers = answers.reshape(-1, cluster)
    struct_pos = answers.at[slot_index].get(mode="promise_in_bounds")
    struct_pos = struct_pos.reshape(fluid_count, 3, cluster // 3)
    mapped = wendland_map(fluid_coords, traction, struct_pos)
    outgoing = jnp.zeros((partitions * capacity, cluster), jnp.float32).at[slot_index].set(mapped)
    outgoing = outgoing.reshape(partitions, capacity, cluster)
    arrived = lax.all_to_all(outgoing, "dom", split_axis=0, concat_axis=0, tiled=True)
    load_field = jnp.dot(
        arrived.reshape(-1, cluster).T,
        onehot,
        precision=lax.Precision.HIGHEST,
        preferred_element_type=jnp.float32,
    )
    found, rest = krylov(load_field, columns, halo_list, blocks, precond)
    return (load_field, found, rest)


def solution(mesh):
    return jax.shard_map(
        on_device,
        mesh=mesh,
        in_specs=(
            P("dom", None, None),
            P("dom", None, None),
            P(None, None, "dom"),
            P("dom", None),
            P("dom"),
            P(None, None, None, "dom"),
            P(None, "dom"),
            P("dom"),
            P(None, None, "dom"),
        ),
        out_specs=(P(None, "dom"), P(None, "dom"), P(None, "dom")),
        check_vma=False,
    )
```

time: 432 us -> 128 us (0.30)
  blocking collectives: 208 us -> 14.3 us
  waiting for transfers between devices: 73.7 us -> 28.1 us
  other arithmetic: 49.7 us -> 4.13 us
  Pallas kernels: 0 us -> 36.4 us
  between operations: 23.9 us -> 0.79 us
  local copies, waits for them, and re-layouts: 30.3 us -> 12.6 us
  starting transfers between devices: 21.6 us -> 5.49 us
    psum x5 -> x0, blocking collectives: 208 us -> none  [the longest x2 84 us: on_device(): lax.psum((jnp.sum(middle_image * middle), jnp.sum(middle_image * middle_i...]
    all_gather x1 -> x0, waiting for transfers between devices: 44 us -> none  [on_device(): all_struct = lax.all_gather(struct_coords, 'dom', axis=2, tiled=True)]
    dot_general x8 -> x0, other arithmetic: 37.4 us -> none  [the longest x4 24.9 us: apply_operator(): jnp.einsum('abi,bi->ai', blocks[neighbor + 1], taken, precision=lax.Preci...]
    pallas_call x0 -> x1, Pallas kernels: none -> 36.4 us  [krylov(): pl.pallas_call(functools.partial(krylov_kernel, parts), out_shape=(field,...]
    ppermute x8 -> x0, waiting for transfers between devices: 14.8 us -> none  [from_behind(): return lax.ppermute(block, axis, route)]
    all_to_all x1, waiting for transfers between devices: 0.01 us -> 14.4 us  [on_device(): lax.all_to_all(asked.reshape(partitions, capacity, cluster), 'dom', split...]
    all_to_all x0 -> x1, blocking collectives: none -> 14.3 us  [on_device(): lax.all_to_all(slot_target, 'dom', split_axis=0, concat_axis=0, tiled=True)]
    gather x13 -> x2, local copies, waits for them, and re-layouts: 12.3 us -> 1.15 us  [on_device(): struct_pos = answers.at[slot_index].get(mode='promise_in_bounds')]
  transfers between devices with their start and end apart: 11 -> 2, of which waited for: 6 -> 2; matrix products, arithmetic and copies ran while one was open for 11% -> 2% of each run, Pallas kernels for 0% -> 0%
where the time goes in v1:
time: 128 us; the launch traced here: 127 us
  Pallas kernels  36.4 us (28%)
  waiting for transfers between devices  28.1 us (22%)
  matrix products  25.6 us (20%)
  blocking collectives  14.3 us (11%)
  local copies, waits for them, and re-layouts  12.6 us (10%)
  starting transfers between devices  5.49 us (4%)
  other arithmetic  4.13 us (3%)
    pallas_call x1, Pallas kernels, krylov(): pl.pallas_call(functools.partial(krylov_kernel, parts), out_shape=(field,...  36.4 us
    dot_general x1, matrix products, wendland_map(): jnp.einsum('bjn,bcn->bcj', weight, force, precision=lax.Precision.HIGHEST)  22.2 us
    all_to_all x1, waiting for transfers between devices, on_device(): lax.all_to_all(asked.reshape(partitions, capacity, cluster), 'dom', split...  14.4 us
    all_to_all x1, blocking collectives, on_device(): lax.all_to_all(slot_target, 'dom', split_axis=0, concat_axis=0, tiled=True)  14.3 us
    all_to_all x1, waiting for transfers between devices, on_device(): lax.all_to_all(outgoing, 'dom', split_axis=0, concat_axis=0, tiled=True)  13.6 us
    all_to_all x1, starting transfers between devices, on_device(): lax.all_to_all(outgoing, 'dom', split_axis=0, concat_axis=0, tiled=True)  2.88 us
    unnamed x6, local copies, waits for them, and re-layouts  2.86 us
    all_to_all x1, starting transfers between devices, on_device(): lax.all_to_all(asked.reshape(partitions, capacity, cluster), 'dom', split...  2.6 us
  transfers between devices with their start and end apart: 2, of which 2 were waited for; matrix products, arithmetic and copies ran while one was open for 2% of the time, Pallas kernels for 0%

profile of v1, /device:TPU:0, one launch (start us, length us, event | category | flops | bytes accessed | tf_op | source)
XLA Modules:
  0.0 127.4 jit_solution(9945419157465623454)
XLA Ops:
  0.6 0.0 copy-start
  0.6 0.8 fusion.43
  1.4 1.2 reduce-window.6
  2.6 0.2 slice_reduce_fusion
  2.8 0.8 fusion.42
  3.6 0.7 compare_select_fusion
  4.3 2.6 %scatter_custom_fusion = s32[1024]{0:T(1024)S(1)} fusion(s32[512]{0:T(512)S(1)} %bitcast.62, s32[512]{0:T(512)} %param.13, s32[]{:T(128)} %constant.9.clone.1), kind=kCustom, calls=%fused_computation.59 | custom fusion | bytes 4608 | tf_op jit(solution)/shard_map/scatter | solution.py:303
  6.9 0.1 all_to_all.12
  7.0 14.3 %all_to_all.19 = s32[32,1,32]{2,1,0:T(1,128)S(1)} all-to-all(s32[32,1,32]{2,1,0:T(1,128)S(1)} %all_to_all.12), channel_id=1, replica_groups=mesh['dom'=32] {'dom'}, dimensions={0} | all-to-all | bytes 8192 | tf_op jit(solution)/shard_map/all_to_all | solution.py:305
  21.3 2.0 %fusion.33 = f32[32,32,96]{2,1,0:T(8,128)} fusion(f32[96,128,1]{1,0,2:T(8,128)} %bitcast.59, s32[32,32]{1,0:T(8,128)S(1)} %bitcast.58), kind=kOutput, calls=%fused_computation.36 | convolution fusion | flops 151126016 | bytes 446464 | tf_op jit(solution)/shard_map/dot_general | solution.py:309
  23.4 2.6 %all-to-all-start.1 = ((f32[32,32,96]{2,1,0:T(8,128)}), f32[32,32,96]{2,1,0:T(8,128)S(1)}, u32[]{:S(2)}, u32[]{:S(2)}) async-start(f32[32,32,96]{2,1,0:T(8,128)} %fusion.33), calls=%async_computation.1 | async-start | bytes 1048576 | tf_op jit(solution)/shard_map/all_to_all | solution.py:315
  26.0 1.2 slice_bitcast_fusion.2
  27.2 14.4 %all-to-all-done.1 = f32[32,32,96]{2,1,0:T(8,128)S(1)} async-done(((f32[32,32,96]{2,1,0:T(8,128)}), f32[32,32,96]{2,1,0:T(8,128)S(1)}, u32[]{:S(2)}, u32[]{:S(2)}) %all-to-all-start.1) | async-done | bytes 393248 | tf_op jit(solution)/shard_map/all_to_all | solution.py:315
  41.6 1.0 gather_fusion
  42.6 0.1 copy.32
  42.8 0.1 copy.33
  42.9 0.1 copy.35
  43.0 0.1 copy.34
  43.2 0.0 copy-done
  43.2 0.0 copy-start.1
  43.2 22.2 %fusion.28 = f32[512,3,32]{2,1,0:T(4,128)S(1)} fusion(f32[512,128]{1,0:T(8,128)S(1)} %get-tuple-element.8, f32[512,32]{1,0:T(8,128)S(1)} %copy.35, f32[512,128]{1,0:T(8,128)S(1)} %get-tuple-element.9, f32[512,32]{1,0:T(8,128)S(1)} %copy.34, f32[512,128]{1,0:T(8,128)S(1)} %get-tuple-element.7, f32[512,32]{1,0:T(8,128)S(1)} %copy.33, ...), kind=kOutput, calls=%fused_computation.31 | convolution fusion | flops 109051904 | bytes 1966080 | tf_op jit(solution)/shard_map/bjn,bcn->bcj/dot_general | solution.py:21
  65.4 0.3 copy.37
  65.7 0.1 copy.38
  65.8 2.5 %scatter_custom_fusion.1 = f32[1024,96]{1,0:T(8,128)} fusion(s32[512]{0:T(512)S(1)} %bitcast.64, f32[512,96]{1,0:T(8,128)S(1)} %copy.38, f32[]{:T(128)} %constant.7.clone.1), kind=kCustom, calls=%fused_computation.43 | custom fusion | bytes 393220 | tf_op jit(solution)/shard_map/scatter | solution.py:326
  68.3 2.9 %all-to-all-start.2 = ((f32[32,32,96]{2,1,0:T(8,128)}), f32[32,32,96]{2,1,0:T(8,128)S(1)}, u32[]{:S(2)}, u32[]{:S(2)}) async-start(f32[32,32,96]{2,1,0:T(8,128)} %bitcast.19), calls=%async_computation.2 | async-start | bytes 1048576 | tf_op jit(solution)/shard_map/all_to_all | solution.py:328
  71.2 0.0 copy-done.1
  71.2 0.7 copy.39.halo_ref
  71.9 0.5 broadcast.70
  72.4 0.7 reduce.5
  73.1 0.1 eq.77
  73.1 13.6 %all-to-all-done.2 = f32[32,32,96]{2,1,0:T(8,128)S(1)} async-done(((f32[32,32,96]{2,1,0:T(8,128)}), f32[32,32,96]{2,1,0:T(8,128)S(1)}, u32[]{:S(2)}, u32[]{:S(2)}) %all-to-all-start.2) | async-done | bytes 393248 | tf_op jit(solution)/shard_map/all_to_all | solution.py:328
  86.8 1.4 %fusion.35.load_ref = f32[96,128]{1,0:T(8,128)} fusion(f32[1024,96]{1,0:T(8,128)S(1)} %bitcast.55, s32[1024]{0:T(1024)S(1)} %eq.77), kind=kOutput, calls=%fused_computation.37 | convolution fusion | flops 151126016 | bytes 446464 | tf_op jit(solution)/shard_map/dot_general | solution.py:329
  88.1 36.4 %krylov.1 = (f32[96,128]{1,0:T(8,128)}, f32[96,128]{1,0:T(8,128)}) custom-call(f32[96,128]{1,0:T(8,128)} %fusion.35.load_ref, s32[2,128]{1,0:T(2,128)} %columns_ref.1, s32[16,1]{1,0:T(8,128)} %copy.39.halo_ref, f32[3,96,96,128]{3,2,1,0:T(8,128)} %blocks_hbm.1, f32[96,96,128]{2,1,0:T(8,128)} %precond_hbm.1), custom_call_target="tpu_custom_call" | custom-call | tf_op jit(solution)/shard_map/krylov/pallas_call | solution.py:264
  124.5 1.4 %copy.46 = f32[96,128]{1,0:T(8,128)} copy(f32[96,128]{1,0:T(8,128)} %get-tuple-element.17) | data formatting | bytes 98304
  126.0 1.4 %copy.47 = f32[96,128]{1,0:T(8,128)} copy(f32[96,128]{1,0:T(8,128)} %get-tuple-element.18) | data formatting | bytes 98304
  (4 shorter events, 0.1 us)
Async XLA Ops:
  0.6 42.5 %copy-start = (f32[512,3,128]{2,0,1:T(8,128)S(1)}, f32[512,3,128]{2,0,1:T(8,128)}, u32[]{:S(2)}) copy-start(f32[512,3,128]{2,0,1:T(8,128)} %param.9) | copy-start | bytes 2359300
  23.4 18.2 %all-to-all-start.1 = ((f32[32,32,96]{2,1,0:T(8,128)}), f32[32,32,96]{2,1,0:T(8,128)S(1)}, u32[]{:S(2)}, u32[]{:S(2)}) async-start(f32[32,32,96]{2,1,0:T(8,128)} %fusion.33), calls=%async_computation.1 | async-start | bytes 1048576 | tf_op jit(solution)/shard_map/all_to_all | solution.py:315
  43.2 28.0 %copy-start.1 = (s32[16]{0:T(128)S(1)}, s32[16]{0:T(128)}, u32[]{:S(2)}) copy-start(s32[16]{0:T(128)} %param.16) | copy-start | bytes 196
  68.3 18.5 %all-to-all-start.2 = ((f32[32,32,96]{2,1,0:T(8,128)}), f32[32,32,96]{2,1,0:T(8,128)S(1)}, u32[]{:S(2)}, u32[]{:S(2)}) async-start(f32[32,32,96]{2,1,0:T(8,128)} %bitcast.19), calls=%async_computation.2 | async-start | bytes 1048576 | tf_op jit(solution)/shard_map/all_to_all | solution.py:328

commit v2 on v1

--- a/solution.py
+++ b/solution.py
@@ -10,18 +10,6 @@
 support = 0.9
 
 
-def wendland_map(fluid_pos, force, struct_pos):
-    dist_sq = jnp.zeros((fluid_pos.shape[0], struct_pos.shape[2], fluid_pos.shape[2]), jnp.float32)
-    for component in range(3):
-        dist_sq = (
-            dist_sq + (struct_pos[:, component, :, None] - fluid_pos[:, component, None, :]) ** 2
-        )
-    radius = jnp.sqrt(dist_sq) / support
-    weight = jnp.maximum(1.0 - radius, 0.0) ** 4 * (4.0 * radius + 1.0)
-    mapped = jnp.einsum("bjn,bcn->bcj", weight, force, precision=lax.Precision.HIGHEST)
-    return mapped.reshape(mapped.shape[0], -1)
-
-
 def split_three(x):
     high = x.astype(jnp.bfloat16)
     rest = x - high.astype(jnp.float32)
@@ -42,11 +30,17 @@
 
 def krylov_kernel(
     parts,
-    load_ref,
+    capacity,
+    traction_ref,
+    fluid_ref,
+    struct_ref,
+    dest_ref,
+    target_ref,
     columns_ref,
     halo_ref,
     blocks_hbm,
     precond_hbm,
+    load_ref,
     solution_ref,
     residual_ref,
     blocks,
@@ -57,6 +51,17 @@
     halo_out,
     halo_in,
     partial,
+    labels_out,
+    labels_in,
+    answers_out,
+    answers_in,
+    mapped_out,
+    mapped_in,
+    struct_pos,
+    mapped,
+    hits,
+    exchange_send,
+    exchange_recv,
     load_sems,
     halo_send,
     halo_recv,
@@ -66,6 +71,8 @@
     me = lax.axis_index("dom")
     cluster, local = load_ref.shape
     listed = halo_ref.shape[0]
+    count = dest_ref.shape[1]
+    nodes = cluster // 3
     barrier = pltpu.get_barrier_semaphore()
 
     loads = [pltpu.make_async_copy(precond_hbm, precond, load_sems.at[0])]
@@ -100,6 +107,130 @@
     send_hot = hot(lax.broadcasted_iota(jnp.int32, (listed, local), 1) == halo_ref[...])
 
     group = 8
+
+    def exchange(turn, source, landing):
+        def copy(outgoing, arriving, target, origin):
+            return pltpu.make_async_remote_copy(
+                src_ref=source.at[outgoing],
+                dst_ref=landing.at[arriving],
+                send_sem=exchange_send.at[turn, target],
+                recv_sem=exchange_recv.at[turn, origin],
+                device_id=(target,),
+                device_id_type=pl.DeviceIdType.MESH,
+            )
+
+        @pl.loop(1, parts)
+        def _(k):
+            peer = lax.rem(me + k, parts)
+            copy(peer, me, peer, me).start()
+
+        landing[me] = source[me]
+
+        @pl.loop(1, parts)
+        def _(k):
+            peer = lax.rem(me + k, parts)
+            copy(peer, peer, peer, peer).wait_recv()
+            copy(peer, me, peer, me).wait_send()
+
+    dest = dest_ref[...]
+    target = target_ref[...]
+    named = lax.broadcasted_iota(jnp.int32, (parts, count), 0) == dest
+    earlier = hot(
+        lax.broadcasted_iota(jnp.int32, (count, count), 0)
+        < lax.broadcasted_iota(jnp.int32, (count, count), 1)
+    )
+    ahead = jnp.dot(hot(named), earlier, preferred_element_type=jnp.float32)
+    rank = jnp.sum(jnp.where(named, ahead, 0.0), axis=0, keepdims=True).astype(jnp.int32)
+    slot_row = dest * capacity + rank
+    marks = jnp.where(named, target.astype(jnp.float32), 0.0).astype(jnp.bfloat16)
+    places = lax.broadcasted_iota(jnp.int32, (local, count), 0)
+    ranked = hot(lax.rem(places, capacity) == rank)
+    asked = lax.dot_general(
+        marks, ranked, (((1,), (1,)), ((), ())), preferred_element_type=jnp.float32
+    )
+    for part in range(parts):
+        labels_out[part] = asked[part : part + 1, :]
+    pl.semaphore_wait(barrier, parts - 1)
+    exchange(0, labels_out, labels_in)
+
+    per_group = local // capacity
+    groups = parts // per_group
+    struct_pieces = split_three(struct_ref[...])
+    lane_owner = lax.broadcasted_iota(jnp.int32, (1, local), 1) // capacity
+    for g in range(groups):
+        row = labels_in[g * per_group]
+        for member in range(1, per_group):
+            row = jnp.where(lane_owner == member, labels_in[g * per_group + member], row)
+        hit = hot(rows == row.astype(jnp.int32))
+        hits[g] = hit
+        found = pick(struct_pieces, hit, ((1,), (0,))).T
+        for member in range(per_group):
+            answers_out[g * per_group + member] = found[
+                member * capacity : (member + 1) * capacity, :
+            ]
+    exchange(1, answers_out, answers_in)
+
+    side = local
+    diagonal = lax.broadcasted_iota(jnp.int32, (side, side), 0) == lax.broadcasted_iota(
+        jnp.int32, (side, side), 1
+    )
+    slots = parts * capacity
+    answers = split_three(answers_in[...].reshape(slots, cluster))
+    for first in range(0, count, side):
+        slot_column = jnp.sum(
+            jnp.where(diagonal, slot_row[:, first : first + side], 0).astype(jnp.float32),
+            axis=1,
+            keepdims=True,
+        ).astype(jnp.int32)
+        chosen = hot(lax.broadcasted_iota(jnp.int32, (side, slots), 1) == slot_column)
+        total = None
+        for piece in answers:
+            term = jnp.dot(chosen, piece, preferred_element_type=jnp.float32)
+            total = term if total is None else total + term
+        struct_pos[first : first + side, :] = total * (1.0 / support)
+
+    @pl.loop(0, count // group)
+    def _(g):
+        start = pl.multiple_of(g * group, group)
+        here = pl.ds(start, group)
+        positions = struct_pos[here, :]
+        fluid = [fluid_ref[c, here, :] * (1.0 / support) for c in range(3)]
+        force = [traction_ref[c, here, :] for c in range(3)]
+        for j in range(nodes):
+            squared = None
+            for c in range(3):
+                offset = positions[:, c * nodes + j : c * nodes + j + 1] - fluid[c]
+                squared = offset * offset if squared is None else squared + offset * offset
+            radius = squared * lax.rsqrt(jnp.maximum(squared, 1e-30))
+            rest = jnp.maximum(1.0 - radius, 0.0)
+            rest = rest * rest
+            weight = rest * rest * (4.0 * radius + 1.0)
+            for c in range(3):
+                mapped[here, c * nodes + j : c * nodes + j + 1] = jnp.sum(
+                    weight * force[c], axis=1, keepdims=True
+                )
+
+    pieces = split_three(mapped[...])
+    for g in range(groups):
+        wanted = hot(
+            lax.broadcasted_iota(jnp.int32, (local, count), 0) + g * local == slot_row
+        )
+        total = None
+        for piece in pieces:
+            term = jnp.dot(wanted, piece, preferred_element_type=jnp.float32)
+            total = term if total is None else total + term
+        for member in range(per_group):
+            mapped_out[g * per_group + member] = total[
+                member * capacity : (member + 1) * capacity, :
+            ]
+    exchange(2, mapped_out, mapped_in)
+    arrived = mapped_in[...].reshape(slots, cluster)
+    load = None
+    for g in range(groups):
+        for piece in split_three(arrived[g * local : (g + 1) * local, :]):
+            term = jnp.dot(hits[g], piece, preferred_element_type=jnp.float32)
+            load = term if load is None else load + term
+    load_ref[...] = load.T
 
     def multiply(matrices, vectors, out_ref):
         @pl.loop(0, cluster // group)
@@ -138,9 +269,6 @@
             )
             outgoing = part if outgoing is None else outgoing + part
         halo_out[step] = outgoing
-        if step == 0:
-            pl.semaphore_wait(barrier, parts - 1)
-
         @pl.when(me < parts - 1)
         def _():
             halo_copy(step, 0).start()
@@ -253,19 +381,24 @@
     residual_ref[...] = (residual - step_size * image) - smoothing * (q - step_size * y)
 
 
-def krylov(load_field, columns, halo_list, blocks, precond):
+def on_device(
+    traction, fluid_coords, struct_coords, dest, target, blocks, columns, halo_list, precond
+):
     parts = lax.axis_size("dom")
-    cluster, local = load_field.shape
+    count = dest.shape[0]
+    cluster = blocks.shape[1]
+    local = blocks.shape[3]
     listed = halo_list.shape[0]
+    capacity = max(2, 2 * count // parts)
     vmem = pl.BlockSpec(memory_space=pltpu.VMEM)
     hbm = pl.BlockSpec(memory_space=pl.ANY)
-    field = jax.ShapeDtypeStruct((cluster, local), jnp.float32)
     f32 = jnp.float32
+    field = jax.ShapeDtypeStruct((cluster, local), f32)
     return pl.pallas_call(
-        functools.partial(krylov_kernel, parts),
-        out_shape=(field, field),
-        in_specs=[vmem, vmem, vmem, hbm, hbm],
-        out_specs=(vmem, vmem),
+        functools.partial(krylov_kernel, parts, capacity),
+        out_shape=(field, field, field),
+        in_specs=[vmem] * 7 + [hbm] * 2,
+        out_specs=(vmem, vmem, vmem),
         scratch_shapes=[
             pltpu.VMEM(blocks.shape, f32),
             pltpu.VMEM(precond.shape, f32),
@@ -275,6 +408,17 @@
             pltpu.VMEM((4, listed, cluster), f32),
             pltpu.VMEM((4, 2, listed, cluster), f32),
             pltpu.VMEM((2, parts, 1, local), f32),
+            pltpu.VMEM((parts, 1, local), f32),
+            pltpu.VMEM((parts, 1, local), f32),
+            pltpu.VMEM((parts, capacity, cluster), f32),
+            pltpu.VMEM((parts, capacity, cluster), f32),
+            pltpu.VMEM((parts, capacity, cluster), f32),
+            pltpu.VMEM((parts, capacity, cluster), f32),
+            pltpu.VMEM((count, cluster), f32),
+            pltpu.VMEM((count, cluster), f32),
+            pltpu.VMEM((parts * capacity // local, local, local), jnp.bfloat16),
+            pltpu.SemaphoreType.DMA((3, parts)),
+            pltpu.SemaphoreType.DMA((3, parts)),
             pltpu.SemaphoreType.DMA((4,)),
             pltpu.SemaphoreType.DMA((4, 2)),
             pltpu.SemaphoreType.DMA((4, 2)),
@@ -282,58 +426,18 @@
             pltpu.SemaphoreType.DMA((2, parts)),
         ],
         compiler_params=pltpu.CompilerParams(collective_id=0, has_side_effects=True),
-        name="krylov",
-    )(load_field, columns, halo_list.reshape(-1, 1), blocks, precond)
-
-
-def on_device(
-    traction, fluid_coords, struct_coords, dest, target, blocks, columns, halo_list, precond
-):
-    partitions = lax.axis_size("dom")
-    fluid_count = dest.shape[0]
-    cluster = blocks.shape[1]
-    local_blocks = blocks.shape[3]
-    capacity = max(2, 2 * fluid_count // partitions)
-    owner_part = dest[:, 0]
-    owner_hits = (owner_part[:, None] == jnp.arange(partitions, dtype=jnp.int32)[None, :]).astype(
-        jnp.int32
-    )
-    before = jnp.sum((jnp.cumsum(owner_hits, axis=0) - owner_hits) * owner_hits, axis=1)
-    slot_index = owner_part * capacity + before
-    slot_target = jnp.zeros((partitions * capacity,), jnp.int32).at[slot_index].set(target)
-    slot_target = slot_target.reshape(partitions, capacity)
-    labels = lax.all_to_all(slot_target, "dom", split_axis=0, concat_axis=0, tiled=True)
-    onehot = (
-        labels.reshape(-1)[:, None] == jnp.arange(local_blocks, dtype=jnp.int32)[None, :]
-    ).astype(jnp.float32)
-    asked = jnp.dot(
-        onehot,
-        struct_coords.reshape(-1, local_blocks).T,
-        precision=lax.Precision.HIGHEST,
-        preferred_element_type=jnp.float32,
-    )
-    answers = lax.all_to_all(
-        asked.reshape(partitions, capacity, cluster),
-        "dom",
-        split_axis=0,
-        concat_axis=0,
-        tiled=True,
-    )
-    answers = answers.reshape(-1, cluster)
-    struct_pos = answers.at[slot_index].get(mode="promise_in_bounds")
-    struct_pos = struct_pos.reshape(fluid_count, 3, cluster // 3)
-    mapped = wendland_map(fluid_coords, traction, struct_pos)
-    outgoing = jnp.zeros((partitions * capacity, cluster), jnp.float32).at[slot_index].set(mapped)
-    outgoing = outgoing.reshape(partitions, capacity, cluster)
-    arrived = lax.all_to_all(outgoing, "dom", split_axis=0, concat_axis=0, tiled=True)
-    load_field = jnp.dot(
-        arrived.reshape(-1, cluster).T,
-        onehot,
-        precision=lax.Precision.HIGHEST,
-        preferred_element_type=jnp.float32,
-    )
-    found, rest = krylov(load_field, columns, halo_list, blocks, precond)
-    return (load_field, found, rest)
+        name="coupling",
+    )(
+        jnp.transpose(traction, (1, 0, 2)),
+        jnp.transpose(fluid_coords, (1, 0, 2)),
+        struct_coords.reshape(cluster, local),
+        dest.reshape(1, count),
+        target.reshape(1, count),
+        columns,
+        halo_list.reshape(-1, 1),
+        blocks,
+        precond,
+    )
 
 
 def solution(mesh):

time: 128 us -> 261 us (2.04)
  Pallas kernels: 36.4 us -> 254 us
  waiting for transfers between devices: 28.1 us -> 0 us
  matrix products: 25.6 us -> 0 us
  blocking collectives: 14.3 us -> 0 us
  local copies, waits for them, and re-layouts: 12.6 us -> 5.59 us
  starting transfers between devices: 5.49 us -> 0 us
  other arithmetic: 4.13 us -> 0 us
    pallas_call x1, Pallas kernels: 36.4 us -> 254 us  [on_device(): pl.pallas_call(functools.partial(krylov_kernel, parts, capacity), out_sha...]
    all_to_all x2 -> x0, waiting for transfers between devices: 28.1 us -> none  [the longest x1 14.4 us: on_device(): lax.all_to_all(asked.reshape(partitions, capacity, cluster), 'dom', split...]
    dot_general x3 -> x0, matrix products: 25.6 us -> none  [the longest x1 22.2 us: wendland_map(): jnp.einsum('bjn,bcn->bcj', weight, force, precision=lax.Precision.HIGHEST)]
    all_to_all x1 -> x0, blocking collectives: 14.3 us -> none  [on_device(): lax.all_to_all(slot_target, 'dom', split_axis=0, concat_axis=0, tiled=True)]
    all_to_all x2 -> x0, starting transfers between devices: 5.49 us -> none  [the longest x1 2.88 us: on_device(): lax.all_to_all(outgoing, 'dom', split_axis=0, concat_axis=0, tiled=True)]
    scatter x2 -> x0, local copies, waits for them, and re-layouts: 5.08 us -> none  [the longest x1 2.6 us: on_device(): jnp.zeros((partitions * capacity,), jnp.int32).at[slot_index].set(target)]
  transfers between devices with their start and end apart: 2 -> 0, of which waited for: 2 -> 0; matrix products, arithmetic and copies ran while one was open for 2% -> 0% of each run, Pallas kernels for 0% -> 0%
where the time goes in v2:
time: 261 us; the launch traced here: 260 us
  Pallas kernels  254 us (97%)
  local copies, waits for them, and re-layouts  5.59 us (2%)
    pallas_call x1, Pallas kernels, on_device(): pl.pallas_call(functools.partial(krylov_kernel, parts, capacity), out_sha...  254 us

profile of v2, /device:TPU:0, one launch (start us, length us, event | category | flops | bytes accessed | tf_op | source)
XLA Modules:
  0.0 260.3 jit_solution(5499202034649278923)
XLA Ops:
  0.6 1.3 copy.12.halo_ref
  2.0 254.1 %coupling.1 = (f32[96,128]{1,0:T(8,128)}, f32[96,128]{1,0:T(8,128)}, f32[96,128]{1,0:T(8,128)}) custom-call(f32[3,512,128]{2,1,0:T(8,128)} %bitcast.6, f32[3,512,128]{2,1,0:T(8,128)} %bitcast.7, f32[96,128]{1,0:T(8,128)} %bitcast.8, s32[1,512]{1,0:T(1,128)} %bitcast.9, s32[1,512]{1,0:T(1,128)} %bitcast.10, s32[2,128]{1,0:T(2,128)} %columns_ref.1, ...), custom_call_target="tpu_custom_call" | custom-call | tf_op jit(solution)/shard_map/coupling/pallas_call | solution.py:397
  256.1 1.4 copy.16
  257.5 1.4 copy.17
  258.9 1.4 copy.18
